TPU v7x, 32 devices: a whole 2x2x4 slice. The times are simulated.
32 devices in a mesh: section: 4 (over y, core), tensor: 8 (over z, x).
Axes of the slice: x: 2, y: 2, z: 4, core: 2. Of those that a mesh axis runs over, the one named last changes fastest.
Arguments:
- saved_inputs: bfloat16 [4, 4, 256, 1024], P('section', None, 'tensor'), may hold values from -6 to 6
- slot_index: int32 [4, 3], P('section'), may hold values from 0 to 3
- example_lengths: int32 [4, 3, 2], P('section'), may hold values from 1 to 192, 256 in all within a row
- first_grads: bfloat16 [4, 256, 1024], P('section', 'tensor'), may hold values from -6 to 6
- loss_grads: bfloat16 [2, 256, 1024], P(None, 'tensor'), may hold values from -6 to 6
- w_in: bfloat16 [4, 1024, 32768], P('section', None, 'tensor'), may hold values from -0.1875 to 0.1875
- w_out: bfloat16 [4, 32768, 1024], P('section', 'tensor'), may hold values from -0.03125 to 0.03125
Outputs:
- grad_in: bfloat16 [4, 1024, 32768], P('section', None, 'tensor')
- grad_out: bfloat16 [4, 32768, 1024], P('section', 'tensor')
- input_grads: bfloat16 [4, 3, 256, 1024], P('section', None, 'tensor')
Inputs may be any that keep to these rules, and one draw needn't show every extreme that they name: `example_lengths`: the 2 lengths of one microbatch sum to 256.
All inputs are finite; a program needn't handle non-finite values.
Results may differ from a plain program's by a relative error of at most 0.0095.
Values may be sent and summed in bfloat16 or wider, within the bound.
A program may use at most 128 MiB of HBM per device.

v0:
```python
import jax
import jax.numpy as jnp
from jax import lax
from jax.sharding import PartitionSpec as P

D = 1024
FF = 32768
GAMMA = 0.01


def shifted(value, axis, steps):
    count = lax.axis_size(axis)
    first, last = (max(0, -steps), min(count, count - steps))
    return lax.ppermute(value, axis, [(source, source + steps) for source in range(first, last)])


def membership(lengths, tokens):
    ends = jnp.cumsum(lengths)
    position = jnp.arange(tokens, dtype=jnp.int32)
    example_id = jnp.sum((position[:, None] >= ends[None, :-1]).astype(jnp.int32), axis=1)
    labels = jnp.arange(lengths.shape[0], dtype=jnp.int32)
    return (example_id[:, None] == labels[None, :]).astype(jnp.float32)


def per_device(saved_inputs, slot_index, example_lengths, first_grads, loss_grads, w_in, w_out):
    section_count = lax.axis_size("section")
    is_last = lax.axis_index("section") == section_count - 1
    first = w_in[0]
    second = w_out[0]
    slot_count = loss_grads.shape[0] + 1
    rows = first_grads.shape[1]
    picked = [
        lax.dynamic_index_in_dim(saved_inputs[0], slot_index[0, slot], 0, keepdims=False)
        for slot in range(slot_count)
    ]
    every_input = lax.all_gather(jnp.stack(picked), "tensor", axis=1, tiled=True)
    acc_first = jnp.zeros(first.shape, jnp.float32)
    acc_second = jnp.zeros(second.shape, jnp.float32)
    incoming = first_grads[0]
    results = []
    for slot in range(slot_count):
        inputs = every_input[slot]
        grads = lax.all_gather(incoming, "tensor", axis=0, tiled=True)
        z = jnp.dot(inputs, first, preferred_element_type=jnp.float32)
        relu = jnp.maximum(z, 0.0)
        hidden = (relu * relu).astype(jnp.bfloat16)
        back = jnp.einsum("td,fd->tf", grads, second, preferred_element_type=jnp.float32)
        dz = (2.0 * relu * back).astype(jnp.bfloat16)
        own_terms = jnp.einsum("tf,df->td", dz, first, preferred_element_type=jnp.float32)
        summed = lax.psum(own_terms, "tensor")
        shares = lax.dynamic_slice_in_dim(summed, lax.axis_index("tensor") * rows, rows, 0)
        member = membership(example_lengths[0, slot], inputs.shape[0])
        pieces = []
        for example in range(member.shape[1]):
            keep = member[:, example][:, None].astype(jnp.bfloat16)
            per_first = jnp.einsum(
                "td,tf->df", inputs * keep, dz, preferred_element_type=jnp.float32
            )
            per_second = jnp.einsum(
                "tf,td->fd", hidden, grads * keep, preferred_element_type=jnp.float32
            )
            pieces.append(jnp.sum(per_first * per_first) + jnp.sum(per_second * per_second))
        local_squares = jnp.stack(pieces)
        squares = lax.psum(local_squares, "tensor")
        factor = 1.0 / (jnp.sqrt(squares / (D * FF)) + GAMMA)
        token_factor = jnp.sum(member * factor[None, :], axis=1)
        dzc = (dz.astype(jnp.float32) * token_factor[:, None]).astype(jnp.bfloat16)
        dyc = (grads.astype(jnp.float32) * token_factor[:, None]).astype(jnp.bfloat16)
        acc_first = acc_first + jnp.einsum(
            "td,tf->df", inputs, dzc, preferred_element_type=jnp.float32
        )
        acc_second = acc_second + jnp.einsum(
            "tf,td->fd", hidden, dyc, preferred_element_type=jnp.float32
        )
        passing = (incoming.astype(jnp.float32) + shares).astype(jnp.bfloat16)
        results.append(passing)
        if slot + 1 < slot_count:
            arrived = shifted(passing, "section", -1)
            incoming = jnp.where(is_last, loss_grads[slot], arrived)
    grad_in = acc_first.astype(jnp.bfloat16)[None]
    grad_out = acc_second.astype(jnp.bfloat16)[None]
    input_grads = jnp.stack(results)[None]
    return (grad_in, grad_out, input_grads)


def solution(mesh):
    return jax.shard_map(
        per_device,
        mesh=mesh,
        in_specs=(
            P("section", None, "tensor", None),
            P("section", None),
            P("section", None, None),
            P("section", "tensor", None),
            P(None, "tensor", None),
            P("section", None, "tensor"),
            P("section", "tensor", None),
        ),
        out_specs=(
            P("section", None, "tensor"),
            P("section", "tensor", None),
            P("section", None, "tensor", None),
        ),
        check_vma=False,
    )
```

profile of v0, /device:TPU:0, one launch (start us, length us, event | category | flops | bytes accessed | tf_op | source)
XLA Modules:
  0.0 492.9 jit_solution(11279649531270042013)
XLA Ops:
  7.2 1.4 fusion.83
  14.4 0.9 dynamic-slice_bitcast_fusion.2
  15.3 0.7 pad_maximum_fusion
  16.1 1.0 slice_reduce_fusion.6
  17.9 34.0 %all-gather = bf16[1,256,1024]{2,1,0:T(8,128)(2,1)S(1)} all-gather(bf16[1,32,1024]{2,1,0:T(8,128)(2,1)} %param.10), channel_id=2, replica_groups=mesh['section'=4,'tensor'=8] {'tensor'}, dimensions={1}, use_global_device_ids=true | all-gather | bytes 589824 | tf_op jit(solution)/shard_map/all_gather | solution.py:43
  51.9 12.3 %all-gather.3.cloned.1.call-done = bf16[3,256,1024]{2,1,0:T(8,128)(2,1)} async-done(((bf16[3,32,1024]{2,1,0:T(8,128)(2,1)}), bf16[3,256,1024]{2,1,0:T(8,128)(2,1)}) %all-gather.3.cloned.1.call-update) | async-done | bytes 1572880 | tf_op jit(solution)/shard_map/all_gather | solution.py:36
  64.2 5.9 %fusion.20 = f32[256,4096]{1,0:T(8,128)S(1)} fusion(bf16[1,1024,4096]{2,1,0:T(8,128)(2,1)} %param.12, bf16[3,256,1024]{2,1,0:T(8,128)(2,1)} %all-gather.3.cloned.1.call-done), kind=kOutput, calls=%fused_computation.34 | convolution fusion | flops 2148532224 | bytes 13107200 | tf_op jit(solution)/shard_map/dot_general | solution.py:44
  70.2 5.2 %multiply_reduce_fusion.8 = f32[]{:T(128)} fusion(bf16[1,256,1024]{2,1,0:T(8,128)(2,1)S(1)} %all-gather, bf16[256]{0:T(256)(128)(2,1)S(1)} %get-tuple-element.11, f32[256,4096]{1,0:T(8,128)S(1)} %fusion.20), kind=kOutput, calls=%fused_computation.10 | convolution fusion | flops 2158231552 | bytes 4719108 | tf_op jit(solution)/shard_map/tf,td->fd/dot_general | solution.py:59
  75.4 5.2 %multiply_reduce_fusion.10 = f32[]{:T(128)} fusion(bf16[1,256,1024]{2,1,0:T(8,128)(2,1)S(1)} %all-gather, bf16[256]{0:T(256)(128)(2,1)S(1)} %get-tuple-element.10, f32[256,4096]{1,0:T(8,128)S(1)} %fusion.20), kind=kOutput, calls=%fused_computation.12 | convolution fusion | flops 2158231552 | bytes 4719108 | tf_op jit(solution)/shard_map/tf,td->fd/dot_general | solution.py:59
  80.6 13.6 %fusion.44 = bf16[256,4096]{1,0:T(8,128)(2,1)S(1)} fusion(bf16[1,4096,1024]{2,1,0:T(8,128)(2,1)S(1)} %bitcast.137, f32[256,4096]{1,0:T(8,128)S(1)} %fusion.20, bf16[1,256,1024]{2,1,0:T(8,128)(2,1)S(1)} %all-gather), kind=kOutput, calls=%fused_computation.42 | convolution fusion | flops 2150629376 | bytes 15204352 | tf_op jit(solution)/shard_map/td,fd->tf/dot_general | solution.py:47
  94.2 7.5 %fusion.12 = f32[256,1024]{1,0:T(8,128)} fusion(bf16[256,4096]{1,0:T(8,128)(2,1)S(1)} %fusion.44, bf16[1,1024,4096]{2,1,0:T(8,128)(2,1)} %param.12), kind=kOutput, calls=%fused_computation.26 | convolution fusion | flops 2147483648 | bytes 11534336 | tf_op jit(solution)/shard_map/tf,df->td/dot_general | solution.py:49
  101.8 6.3 %multiply_reduce_fusion.9 = f32[]{:T(128)} fusion(bf16[256,4096]{1,0:T(8,128)(2,1)S(1)} %fusion.44, bf16[3,256,1024]{2,1,0:T(8,128)(2,1)} %all-gather.3.cloned.1.call-done, bf16[256]{0:T(256)(128)(2,1)S(1)} %get-tuple-element.11), kind=kOutput, calls=%fused_computation.11 | convolution fusion | flops 2156134400 | bytes 2621956 | tf_op jit(solution)/shard_map/td,tf->df/dot_general | solution.py:56
  109.4 6.3 %multiply_reduce_fusion.11 = f32[]{:T(128)} fusion(bf16[256,4096]{1,0:T(8,128)(2,1)S(1)} %fusion.44, bf16[3,256,1024]{2,1,0:T(8,128)(2,1)} %all-gather.3.cloned.1.call-done, bf16[256]{0:T(256)(128)(2,1)S(1)} %get-tuple-element.10), kind=kOutput, calls=%fused_computation.13 | convolution fusion | flops 2156134400 | bytes 2621956 | tf_op jit(solution)/shard_map/td,tf->df/dot_general | solution.py:56
  117.0 8.0 %fusion.26 = f32[256,4096]{1,0:T(8,128)} fusion(bf16[1,1024,4096]{2,1,0:T(8,128)(2,1)} %param.12, bf16[3,256,1024]{2,1,0:T(8,128)(2,1)} %all-gather.3.cloned.1.call-done), kind=kOutput, calls=%fused_computation.36 | convolution fusion | flops 2148532224 | bytes 13107200 | tf_op jit(solution)/shard_map/dot_general | solution.py:44
  125.0 8.5 %fusion.23 = f32[256,4096]{1,0:T(8,128)} fusion(bf16[1,1024,4096]{2,1,0:T(8,128)(2,1)} %param.12, bf16[3,256,1024]{2,1,0:T(8,128)(2,1)} %all-gather.3.cloned.1.call-done), kind=kOutput, calls=%fused_computation.35 | convolution fusion | flops 2148532224 | bytes 13107200 | tf_op jit(solution)/shard_map/dot_general | solution.py:44
  133.5 45.7 %all-reduce.5.cloned.1.call-done = f32[256,1024]{1,0:T(8,128)} async-done(((f32[256,1024]{1,0:T(8,128)}), f32[256,1024]{1,0:T(8,128)}) %all-reduce.5.cloned.1.call-update) | async-done | bytes 1048592 | tf_op jit(solution)/shard_map/psum | solution.py:50
  179.2 0.9 fusion.81
  180.1 1.3 collective-permute-start
  181.5 1.8 collective-permute-done
  183.2 31.3 %all_gather.14 = bf16[256,1024]{1,0:T(8,128)(2,1)S(1)} all-gather(bf16[32,1024]{1,0:T(8,128)(2,1)S(1)} %bitcast_select_fusion.1), channel_id=1, replica_groups=mesh['section'=4,'tensor'=8] {'tensor'}, dimensions={0}, use_global_device_ids=true | all-gather | bytes 589824 | tf_op jit(solution)/shard_map/all_gather | solution.py:43
  214.5 7.2 %fusion.41 = bf16[256,4096]{1,0:T(8,128)(2,1)S(1)} fusion(bf16[256,1024]{1,0:T(8,128)(2,1)S(1)} %all_gather.14, bf16[1,4096,1024]{2,1,0:T(8,128)(2,1)} %param.13, f32[256,4096]{1,0:T(8,128)} %fusion.23), kind=kOutput, calls=%fused_computation.41 | convolution fusion | flops 2150629376 | bytes 15204352 | tf_op jit(solution)/shard_map/td,fd->tf/dot_general | solution.py:47
  221.8 5.2 %multiply_reduce_fusion.4 = f32[]{:T(128)} fusion(bf16[256,1024]{1,0:T(8,128)(2,1)S(1)} %all_gather.14, bf16[256]{0:T(256)(128)(2,1)S(1)} %get-tuple-element.9, f32[256,4096]{1,0:T(8,128)S(1)} %copy-done.2), kind=kOutput, calls=%fused_computation.6 | convolution fusion | flops 2158231552 | bytes 4719108 | tf_op jit(solution)/shard_map/tf,td->fd/dot_general | solution.py:59
  226.9 6.8 %fusion.8 = f32[256,1024]{1,0:T(8,128)} fusion(bf16[256,4096]{1,0:T(8,128)(2,1)S(1)} %fusion.41, bf16[1,1024,4096]{2,1,0:T(8,128)(2,1)} %param.12), kind=kOutput, calls=%fused_computation.22 | convolution fusion | flops 2147483648 | bytes 11534336 | tf_op jit(solution)/shard_map/tf,df->td/dot_general | solution.py:49
  233.7 0.2 all-reduce.9.cloned.1.call-start
  234.0 6.3 %multiply_reduce_fusion.5 = f32[]{:T(128)} fusion(bf16[256,4096]{1,0:T(8,128)(2,1)S(1)} %fusion.41, bf16[3,256,1024]{2,1,0:T(8,128)(2,1)} %all-gather.3.cloned.1.call-done, bf16[256]{0:T(256)(128)(2,1)S(1)} %get-tuple-element.9), kind=kOutput, calls=%fused_computation.7 | convolution fusion | flops 2156134400 | bytes 2621956 | tf_op jit(solution)/shard_map/td,tf->df/dot_general | solution.py:56
  241.5 6.5 %multiply_reduce_fusion.7 = f32[]{:T(128)} fusion(bf16[256,4096]{1,0:T(8,128)(2,1)S(1)} %fusion.41, bf16[3,256,1024]{2,1,0:T(8,128)(2,1)} %all-gather.3.cloned.1.call-done, bf16[256]{0:T(256)(128)(2,1)S(1)} %get-tuple-element.8), kind=kOutput, calls=%fused_computation.9 | convolution fusion | flops 2156134400 | bytes 2621956 | tf_op jit(solution)/shard_map/td,tf->df/dot_general | solution.py:56
  248.0 5.6 %multiply_reduce_fusion.6 = f32[]{:T(128)} fusion(bf16[256,1024]{1,0:T(8,128)(2,1)S(1)} %all_gather.14, bf16[256]{0:T(256)(128)(2,1)S(1)} %get-tuple-element.8, f32[256,4096]{1,0:T(8,128)S(1)} %copy-done.3), kind=kOutput, calls=%fused_computation.8 | convolution fusion | flops 2158231552 | bytes 4719108 | tf_op jit(solution)/shard_map/tf,td->fd/dot_general | solution.py:59
  254.9 57.6 %all-reduce.7.cloned.1.call-done = f32[256,1024]{1,0:T(8,128)} async-done(((f32[256,1024]{1,0:T(8,128)}), f32[256,1024]{1,0:T(8,128)}) %all-reduce.7.cloned.1.call-update) | async-done | bytes 1048592 | tf_op jit(solution)/shard_map/psum | solution.py:50
  312.5 0.9 add_convert_fusion.3
  313.4 1.3 collective-permute-start.1
  314.8 1.8 collective-permute-done.1
  316.6 31.3 %all_gather.15 = bf16[256,1024]{1,0:T(8,128)(2,1)S(1)} all-gather(bf16[32,1024]{1,0:T(8,128)(2,1)S(1)} %bitcast_select_fusion), channel_id=1, replica_groups=mesh['section'=4,'tensor'=8] {'tensor'}, dimensions={0}, use_global_device_ids=true | all-gather | bytes 589824 | tf_op jit(solution)/shard_map/all_gather | solution.py:43
  347.9 7.1 %fusion.38 = bf16[256,4096]{1,0:T(8,128)(2,1)S(1)} fusion(bf16[256,1024]{1,0:T(8,128)(2,1)S(1)} %all_gather.15, bf16[1,4096,1024]{2,1,0:T(8,128)(2,1)} %param.13, f32[256,4096]{1,0:T(8,128)} %fusion.26), kind=kOutput, calls=%fused_computation.40 | convolution fusion | flops 2150629376 | bytes 15204352 | tf_op jit(solution)/shard_map/td,fd->tf/dot_general | solution.py:47
  355.0 5.2 %multiply_reduce_fusion = f32[]{:T(128)} fusion(bf16[256,1024]{1,0:T(8,128)(2,1)S(1)} %all_gather.15, bf16[256]{0:T(256)(128)(2,1)S(1)} %get-tuple-element.4, f32[256,4096]{1,0:T(8,128)S(1)} %copy-done.4), kind=kOutput, calls=%fused_computation.2 | convolution fusion | flops 2158231552 | bytes 4719108 | tf_op jit(solution)/shard_map/tf,td->fd/dot_general | solution.py:59
  360.2 5.2 %multiply_reduce_fusion.2 = f32[]{:T(128)} fusion(bf16[256,1024]{1,0:T(8,128)(2,1)S(1)} %all_gather.15, bf16[256]{0:T(256)(128)(2,1)S(1)} %get-tuple-element.3, f32[256,4096]{1,0:T(8,128)S(1)} %copy-done.4), kind=kOutput, calls=%fused_computation.4 | convolution fusion | flops 2158231552 | bytes 4719108 | tf_op jit(solution)/shard_map/tf,td->fd/dot_general | solution.py:59
  365.4 6.5 %multiply_reduce_fusion.1 = f32[]{:T(128)} fusion(bf16[256,4096]{1,0:T(8,128)(2,1)S(1)} %fusion.38, bf16[3,256,1024]{2,1,0:T(8,128)(2,1)} %all-gather.3.cloned.1.call-done, bf16[256]{0:T(256)(128)(2,1)S(1)} %get-tuple-element.4), kind=kOutput, calls=%fused_computation.3 | convolution fusion | flops 2156134400 | bytes 2621956 | tf_op jit(solution)/shard_map/td,tf->df/dot_general | solution.py:56
  373.1 6.3 %multiply_reduce_fusion.3 = f32[]{:T(128)} fusion(bf16[256,4096]{1,0:T(8,128)(2,1)S(1)} %fusion.38, bf16[3,256,1024]{2,1,0:T(8,128)(2,1)} %all-gather.3.cloned.1.call-done, bf16[256]{0:T(256)(128)(2,1)S(1)} %get-tuple-element.3), kind=kOutput, calls=%fused_computation.5 | convolution fusion | flops 2156134400 | bytes 2621956 | tf_op jit(solution)/shard_map/td,tf->df/dot_general | solution.py:56
  380.7 6.7 %fusion.6 = f32[256,1024]{1,0:T(8,128)} fusion(bf16[256,4096]{1,0:T(8,128)(2,1)S(1)} %fusion.38, bf16[1,1024,4096]{2,1,0:T(8,128)(2,1)} %param.12), kind=kOutput, calls=%fused_computation.20 | convolution fusion | flops 2147483648 | bytes 11534336 | tf_op jit(solution)/shard_map/tf,df->td/dot_general | solution.py:49
  387.5 20.4 %all-reduce = (f32[2]{0:T(128)S(1)}, f32[2]{0:T(128)S(1)}, f32[2]{0:T(128)S(1)}) all-reduce(f32[2]{0:T(128)S(1)} %pad_maximum_fusion.1, f32[2]{0:T(128)S(1)} %pad_maximum_fusion.2, f32[2]{0:T(128)S(1)} %pad_maximum_fusion.3), channel_id=1, replica_groups=mesh['section'=4,'tensor'=8] {'tensor'}, use_global_device_ids=true, to_apply=%region_5.6 | all-reduce | flops 6 | bytes 48 | tf_op jit(solution)/shard_map/psum | solution.py:64
  408.2 10.6 %fusion.53 = f32[4096,1024]{1,0:T(8,128)} fusion(bf16[256,1024]{1,0:T(8,128)(2,1)} %copy-done.5, f32[256]{0:T(256)S(1)} %select_reduce_fusion.1, f32[256,4096]{1,0:T(8,128)} %fusion.23), kind=kOutput, calls=%fused_computation.58 | convolution fusion | flops 2150367232 | bytes 21496832 | tf_op jit(solution)/shard_map/tf,td->fd/dot_general | solution.py:72
  418.8 8.2 %fusion.52 = f32[4096,1024]{1,0:T(8,128)} fusion(bf16[1,256,1024]{2,1,0:T(8,128)(2,1)S(1)} %all-gather, f32[256]{0:T(256)S(1)} %select_reduce_fusion.2, f32[256,4096]{1,0:T(8,128)S(1)} %copy-done.1), kind=kOutput, calls=%fused_computation.57 | convolution fusion | flops 2150367232 | bytes 21496832 | tf_op jit(solution)/shard_map/tf,td->fd/dot_general | solution.py:72
  427.0 16.7 %fusion.19 = bf16[1,4096,1024]{2,1,0:T(8,128)(2,1)} fusion(f32[4096,1024]{1,0:T(8,128)} %fusion.52, f32[4096,1024]{1,0:T(8,128)} %fusion.53, bf16[256,1024]{1,0:T(8,128)(2,1)S(1)} %all_gather.15, f32[256]{0:T(256)S(1)} %select_reduce_fusion, f32[256,4096]{1,0:T(8,128)} %fusion.26), kind=kOutput, calls=%fused_computation.33 | convolution fusion | flops 2162950144 | bytes 46662656 | tf_op jit(solution)/shard_map/tf,td->fd/dot_general | solution.py:72
  443.8 10.1 %fusion.47 = f32[1024,4096]{1,0:T(8,128)} fusion(bf16[256,4096]{1,0:T(8,128)(2,1)} %copy-done.6, f32[256]{0:T(256)S(1)} %select_reduce_fusion.2, bf16[3,256,1024]{2,1,0:T(8,128)(2,1)} %all-gather.3.cloned.1.call-done), kind=kOutput, calls=%fused_computation.49 | convolution fusion | flops 2150629376 | bytes 19399680 | tf_op jit(solution)/shard_map/td,tf->df/dot_general | solution.py:69
  453.9 9.3 %fusion.48 = f32[1024,4096]{1,0:T(8,128)} fusion(bf16[256,4096]{1,0:T(8,128)(2,1)S(1)} %copy-done.8, f32[256]{0:T(256)S(1)} %select_reduce_fusion.1, bf16[3,256,1024]{2,1,0:T(8,128)(2,1)} %all-gather.3.cloned.1.call-done), kind=kOutput, calls=%fused_computation.50 | convolution fusion | flops 2150629376 | bytes 19399680 | tf_op jit(solution)/shard_map/td,tf->df/dot_general | solution.py:69
  463.1 16.0 %fusion.18 = bf16[1,1024,4096]{2,1,0:T(8,128)(2,1)} fusion(f32[1024,4096]{1,0:T(8,128)} %fusion.47, f32[1024,4096]{1,0:T(8,128)} %fusion.48, bf16[256,4096]{1,0:T(8,128)(2,1)S(1)} %fusion.38, f32[256]{0:T(256)S(1)} %select_reduce_fusion, bf16[3,256,1024]{2,1,0:T(8,128)(2,1)} %all-gather.3.cloned.1.call-done), kind=kOutput, calls=%fused_computation.32 | convolution fusion | flops 2163212288 | bytes 44565504 | tf_op jit(solution)/shard_map/td,tf->df/dot_general | solution.py:69
  479.2 5.2 %all-reduce.9.cloned.1.call-done = f32[256,1024]{1,0:T(8,128)} async-done(((f32[256,1024]{1,0:T(8,128)}), f32[256,1024]{1,0:T(8,128)}) %all-reduce.9.cloned.1.call-update) | async-done | bytes 1048592 | tf_op jit(solution)/shard_map/psum | solution.py:50
  484.3 0.9 fusion.82
  485.2 0.7 maximum_bitcast_fusion
  (56 shorter events, 1.5 us)
Async XLA Ops:
  7.2 57.0 %all-gather.3.cloned.1.call-start = ((), (), s32[]{:S(2)}) async-start(), calls=%async_computation | async-start | bytes 1769472 | tf_op jit(solution)/shard_map/all_gather | solution.py:36
  16.0 163.1 %all-reduce.5.cloned.1.call-start = ((), (), s32[]{:S(2)}) async-start(), calls=%async_computation.1 | async-start | bytes 2097152 | tf_op jit(solution)/shard_map/psum | solution.py:50
  70.1 10.4 %copy-start = (f32[256,4096]{1,0:T(8,128)}, f32[256,4096]{1,0:T(8,128)S(1)}, u32[]{:S(2)}) copy-start(f32[256,4096]{1,0:T(8,128)S(1)} %fusion.20) | copy-start | bytes 12582916
  70.2 10.4 %slice-start = ((s8[8388608]{0:T(1024)(128)(4,1)}), s8[4194304]{0:T(1024)(128)(4,1)S(1)}, s32[]{:S(2)}) async-start(s8[8388608]{0:T(1024)(128)(4,1)} %bitcast.136), calls=%async_computation.4 | async-start | bytes 8388608
  75.4 5.2 %slice-start.1 = ((s8[8388608]{0:T(1024)(128)(4,1)}), s8[4194304]{0:T(1024)(128)(4,1)S(1)}, s32[]{:S(2)}) async-start(s8[8388608]{0:T(1024)(128)(4,1)} %bitcast.136), calls=%async_computation.5 | async-start | bytes 8388608
  94.2 15.2 %copy-start.6 = (bf16[256,4096]{1,0:T(8,128)(2,1)}, bf16[256,4096]{1,0:T(8,128)(2,1)S(1)}, u32[]{:S(2)}) copy-start(bf16[256,4096]{1,0:T(8,128)(2,1)S(1)} %fusion.44) | copy-start | bytes 6291460
  101.7 210.8 %all-reduce.7.cloned.1.call-start = ((), (), s32[]{:S(2)}) async-start(), calls=%async_computation.2 | async-start | bytes 2097152 | tf_op jit(solution)/shard_map/psum | solution.py:50
  125.0 54.2 %copy-start.9 = (bf16[1,32,1024]{2,1,0:T(8,128)(2,1)S(1)}, bf16[1,32,1024]{2,1,0:T(8,128)(2,1)}, u32[]{:S(2)}) copy-start(bf16[1,32,1024]{2,1,0:T(8,128)(2,1)} %param.10) | copy-start | bytes 196612
  125.0 58.3 %copy-start.10 = (bf16[2,32,1024]{2,1,0:T(8,128)(2,1)S(1)}, bf16[2,32,1024]{2,1,0:T(8,128)(2,1)}, u32[]{:S(2)}) copy-start(bf16[2,32,1024]{2,1,0:T(8,128)(2,1)} %param.11) | copy-start | bytes 393220
  180.1 3.1 collective-permute-start
  214.5 33.5 %copy-start.5 = (bf16[256,1024]{1,0:T(8,128)(2,1)}, bf16[256,1024]{1,0:T(8,128)(2,1)S(1)}, u32[]{:S(2)}) copy-start(bf16[256,1024]{1,0:T(8,128)(2,1)S(1)} %all_gather.14) | copy-start | bytes 1572868
  214.5 7.2 %copy-start.2 = (f32[256,4096]{1,0:T(8,128)S(1)}, f32[256,4096]{1,0:T(8,128)}, u32[]{:S(2)}) copy-start(f32[256,4096]{1,0:T(8,128)} %fusion.23) | copy-start | bytes 12582916
  221.7 19.7 %copy-start.7 = (bf16[256,4096]{1,0:T(8,128)(2,1)}, bf16[256,4096]{1,0:T(8,128)(2,1)S(1)}, u32[]{:S(2)}) copy-start(bf16[256,4096]{1,0:T(8,128)(2,1)S(1)} %fusion.41) | copy-start | bytes 6291460
  233.7 250.6 %all-reduce.9.cloned.1.call-start = ((), (), s32[]{:S(2)}) async-start(), calls=%async_computation.3 | async-start | bytes 2097152 | tf_op jit(solution)/shard_map/psum | solution.py:50
  241.5 6.5 %copy-start.3 = (f32[256,4096]{1,0:T(8,128)S(1)}, f32[256,4096]{1,0:T(8,128)}, u32[]{:S(2)}) copy-start(f32[256,4096]{1,0:T(8,128)} %fusion.23) | copy-start | bytes 12582916
  313.4 3.1 collective-permute-start.1
  347.9 7.1 %copy-start.4 = (f32[256,4096]{1,0:T(8,128)S(1)}, f32[256,4096]{1,0:T(8,128)}, u32[]{:S(2)}) copy-start(f32[256,4096]{1,0:T(8,128)} %fusion.26) | copy-start | bytes 12582916
  408.2 10.6 %copy-start.1 = (f32[256,4096]{1,0:T(8,128)S(1)}, f32[256,4096]{1,0:T(8,128)}, u32[]{:S(2)}) copy-start(f32[256,4096]{1,0:T(8,128)} %copy-done) | copy-start | bytes 12582916
  443.8 10.1 %copy-start.8 = (bf16[256,4096]{1,0:T(8,128)(2,1)S(1)}, bf16[256,4096]{1,0:T(8,128)(2,1)}, u32[]{:S(2)}) copy-start(bf16[256,4096]{1,0:T(8,128)(2,1)} %copy-done.7) | copy-start | bytes 6291460
Sparse Core Ops, SparseCore 0:
  16.2 48.0 all-gather.2
  101.8 77.2 all-reduce.4
  233.8 78.5 all-reduce.6
  408.3 75.9 all-reduce.8
where the time goes:
time: 503 us; the launch traced here: 493 us
  matrix products  212 us (42%)
  waiting for transfers between devices  124 us (25%)
  blocking collectives  117 us (23%)
  between operations  27.8 us (6%)
  other arithmetic  5.36 us (1%)
    psum x3, waiting for transfers between devices, per_device(): summed = lax.psum(own_terms, 'tensor')  108 us
    all_gather x3, blocking collectives, per_device(): grads = lax.all_gather(incoming, 'tensor', axis=0, tiled=True)  96.6 us
    dot_general x6, matrix products, per_device(): jnp.einsum('td,tf->df', inputs * keep, dz, preferred_element_type=jnp.flo...  38.2 us
    dot_general x3, matrix products, per_device(): jnp.einsum('tf,td->fd', hidden, dyc, preferred_element_type=jnp.float32)  35.6 us
    dot_general x3, matrix products, per_device(): jnp.einsum('td,tf->df', inputs, dzc, preferred_element_type=jnp.float32)  35.4 us
    dot_general x6, matrix products, per_device(): jnp.einsum('tf,td->fd', hidden, grads * keep, preferred_element_type=jnp....  31.6 us
    dot_general x3, matrix products, per_device(): jnp.einsum('td,fd->tf', grads, second, preferred_element_type=jnp.float32)  27.9 us
    dot_general x3, matrix products, per_device(): z = jnp.dot(inputs, first, preferred_element_type=jnp.float32)  22.4 us
  transfers between devices with their start and end apart: 6, of which 6 were waited for; matrix products, arithmetic and copies ran while one was open for 24% of the time, Pallas kernels for 0%

commit v1 on v0

--- a/solution.py
+++ b/solution.py
@@ -47,7 +47,9 @@
         back = jnp.einsum("td,fd->tf", grads, second, preferred_element_type=jnp.float32)
         dz = (2.0 * relu * back).astype(jnp.bfloat16)
         own_terms = jnp.einsum("tf,df->td", dz, first, preferred_element_type=jnp.float32)
-        summed = lax.psum(own_terms, "tensor")
+        summed = own_terms
+        for hop in (1, 2, 4):
+            summed = summed + lax.ppermute(summed, "tensor", [(dev, dev ^ hop) for dev in range(8)])
         shares = lax.dynamic_slice_in_dim(summed, lax.axis_index("tensor") * rows, rows, 0)
         member = membership(example_lengths[0, slot], inputs.shape[0])
         pieces = []

time: 503 us -> 521 us (1.036)
  waiting for transfers between devices: 124 us -> 151 us
  matrix products: 212 us -> 192 us
  starting transfers between devices: 2.93 us -> 9.57 us
  other arithmetic: 5.36 us -> 11.2 us
    ppermute x0 -> x9, waiting for transfers between devices: none -> 135 us  [per_device(): lax.ppermute(summed, 'tensor', [(dev, dev ^ hop) for dev in range(8)])]
    psum x3 -> x0, waiting for transfers between devices: 108 us -> none  [per_device(): summed = lax.psum(own_terms, 'tensor')]
    dot_general x3, matrix products: 27.9 us -> 17 us  [per_device(): jnp.einsum('td,fd->tf', grads, second, preferred_element_type=jnp.float32)]
    add x0 -> x6, other arithmetic: none -> 7.58 us  [per_device(): summed + lax.ppermute(summed, 'tensor', [(dev, dev ^ hop) for dev in rang...]
    ppermute x0 -> x9, starting transfers between devices: none -> 6.68 us  [per_device(): lax.ppermute(summed, 'tensor', [(dev, dev ^ hop) for dev in range(8)])]
    dot_general x3, matrix products: 22.4 us -> 16.6 us  [per_device(): z = jnp.dot(inputs, first, preferred_element_type=jnp.float32)]
  transfers between devices with their start and end apart: 6 -> 12, of which waited for: 6 -> 9; matrix products, arithmetic and copies ran while one was open for 24% -> 25% of each run, Pallas kernels for 0% -> 0%
where the time goes in v1:
time: 521 us; the launch traced here: 512 us
  matrix products  192 us (37%)
  waiting for transfers between devices  151 us (29%)
  blocking collectives  117 us (22%)
  between operations  28.4 us (5%)
  other arithmetic  11.2 us (2%)
  starting transfers between devices  9.57 us (2%)
    ppermute x9, waiting for transfers between devices, per_device(): lax.ppermute(summed, 'tensor', [(dev, dev ^ hop) for dev in range(8)])  135 us
    all_gather x3, blocking collectives, per_device(): grads = lax.all_gather(incoming, 'tensor', axis=0, tiled=True)  97.1 us
    dot_general x6, matrix products, per_device(): jnp.einsum('td,tf->df', inputs * keep, dz, preferred_element_type=jnp.flo...  37.7 us
    dot_general x3, matrix products, per_device(): jnp.einsum('tf,td->fd', hidden, dyc, preferred_element_type=jnp.float32)  35.4 us
    dot_general x3, matrix products, per_device(): jnp.einsum('td,tf->df', inputs, dzc, preferred_element_type=jnp.float32)  34.3 us
    dot_general x6, matrix products, per_device(): jnp.einsum('tf,td->fd', hidden, grads * keep, preferred_element_type=jnp....  34 us
    psum x1, blocking collectives, per_device(): squares = lax.psum(local_squares, 'tensor')  19.8 us
    dot_general x3, matrix products, per_device(): jnp.einsum('td,fd->tf', grads, second, preferred_element_type=jnp.float32)  17 us
  transfers between devices with their start and end apart: 12, of which 9 were waited for; matrix products, arithmetic and copies ran while one was open for 25% of the time, Pallas kernels for 0%

profile of v1, /device:TPU:0, one launch (start us, length us, event | category | flops | bytes accessed | tf_op | source)
XLA Modules:
  0.0 512.1 jit_solution(15997401446273757355)
XLA Ops:
  7.2 1.4 fusion.88
  16.0 33.8 %all-gather = bf16[1,256,1024]{2,1,0:T(8,128)(2,1)S(1)} all-gather(bf16[1,32,1024]{2,1,0:T(8,128)(2,1)} %param.10), channel_id=2, replica_groups=mesh['section'=4,'tensor'=8] {'tensor'}, dimensions={1}, use_global_device_ids=true | all-gather | bytes 589824 | tf_op jit(solution)/shard_map/all_gather | solution.py:43
  49.8 14.1 %all-gather.3.cloned.1.call-done = bf16[3,256,1024]{2,1,0:T(8,128)(2,1)} async-done(((bf16[3,32,1024]{2,1,0:T(8,128)(2,1)}), bf16[3,256,1024]{2,1,0:T(8,128)(2,1)}) %all-gather.3.cloned.1.call-update) | async-done | bytes 1572880 | tf_op jit(solution)/shard_map/all_gather | solution.py:36
  63.9 6.0 %fusion.20 = f32[256,4096]{1,0:T(8,128)S(1)} fusion(bf16[1,1024,4096]{2,1,0:T(8,128)(2,1)} %param.12, bf16[3,256,1024]{2,1,0:T(8,128)(2,1)} %all-gather.3.cloned.1.call-done), kind=kOutput, calls=%fused_computation.34 | convolution fusion | flops 2148532224 | bytes 13107200 | tf_op jit(solution)/shard_map/dot_general | solution.py:44
  70.0 7.4 %fusion.44 = bf16[256,4096]{1,0:T(8,128)(2,1)S(1)} fusion(bf16[1,4096,1024]{2,1,0:T(8,128)(2,1)} %param.13, f32[256,4096]{1,0:T(8,128)S(1)} %fusion.20, bf16[1,256,1024]{2,1,0:T(8,128)(2,1)S(1)} %all-gather), kind=kOutput, calls=%fused_computation.42 | convolution fusion | flops 2150629376 | bytes 15204352 | tf_op jit(solution)/shard_map/td,fd->tf/dot_general | solution.py:47
  77.4 3.3 fusion.12
  82.3 22.7 %collective-permute-done = f32[256,1024]{1,0:T(8,128)} collective-permute-done((f32[256,1024]{1,0:T(8,128)}, f32[256,1024]{1,0:T(8,128)}, u32[]{:S(2)}, u32[]{:S(2)}) %collective-permute-start) | collective-permute-done | bytes 1048608 | tf_op jit(solution)/shard_map/ppermute | solution.py:52
  105.0 1.7 add.102
  106.7 1.3 collective-permute-start.1
  108.1 7.5 %multiply_reduce_fusion.8 = f32[]{:T(128)} fusion(bf16[1,256,1024]{2,1,0:T(8,128)(2,1)S(1)} %all-gather, bf16[256]{0:T(256)(128)(2,1)S(1)} %get-tuple-element.11, f32[256,4096]{1,0:T(8,128)} %copy-done), kind=kOutput, calls=%fused_computation.10 | convolution fusion | flops 2158231552 | bytes 4719108 | tf_op jit(solution)/shard_map/tf,td->fd/dot_general | solution.py:61
  115.6 14.1 %collective-permute-done.1 = f32[256,1024]{1,0:T(8,128)S(1)} collective-permute-done((f32[256,1024]{1,0:T(8,128)S(1)}, f32[256,1024]{1,0:T(8,128)S(1)}, u32[]{:S(2)}, u32[]{:S(2)}) %collective-permute-start.1) | collective-permute-done | bytes 1048608 | tf_op jit(solution)/shard_map/ppermute | solution.py:52
  129.9 2.4 collective-permute-start.2
  132.3 5.5 %multiply_reduce_fusion.10 = f32[]{:T(128)} fusion(bf16[1,256,1024]{2,1,0:T(8,128)(2,1)S(1)} %all-gather, bf16[256]{0:T(256)(128)(2,1)S(1)} %get-tuple-element.10, f32[256,4096]{1,0:T(8,128)S(1)} %copy-done.1), kind=kOutput, calls=%fused_computation.12 | convolution fusion | flops 2158231552 | bytes 4719108 | tf_op jit(solution)/shard_map/tf,td->fd/dot_general | solution.py:61
  137.9 2.4 fusion.23
  140.3 35.2 %collective-permute-done.2 = f32[256,1024]{1,0:T(8,128)S(1)} collective-permute-done((f32[256,1024]{1,0:T(8,128)S(1)}, f32[256,1024]{1,0:T(8,128)S(1)}, u32[]{:S(2)}, u32[]{:S(2)}) %collective-permute-start.2) | collective-permute-done | bytes 1048608 | tf_op jit(solution)/shard_map/ppermute | solution.py:52
  175.6 1.6 collective-permute-start.3
  177.2 5.3 %multiply_reduce_fusion.9 = f32[]{:T(128)} fusion(bf16[256,4096]{1,0:T(8,128)(2,1)S(1)} %fusion.44, bf16[3,256,1024]{2,1,0:T(8,128)(2,1)S(1)} %copy-done.14, bf16[256]{0:T(256)(128)(2,1)S(1)} %get-tuple-element.11), kind=kOutput, calls=%fused_computation.11 | convolution fusion | flops 2156134400 | bytes 2621956 | tf_op jit(solution)/shard_map/td,tf->df/dot_general | solution.py:58
  182.4 31.9 %all_gather.14 = bf16[256,1024]{1,0:T(8,128)(2,1)S(1)} all-gather(bf16[32,1024]{1,0:T(8,128)(2,1)S(1)} %bitcast_select_fusion.1), channel_id=1, replica_groups=mesh['section'=4,'tensor'=8] {'tensor'}, dimensions={0}, use_global_device_ids=true | all-gather | bytes 589824 | tf_op jit(solution)/shard_map/all_gather | solution.py:43
  214.4 2.5 fusion.41
  216.9 6.5 %fusion.8 = f32[256,1024]{1,0:T(8,128)S(1)} fusion(bf16[256,4096]{1,0:T(8,128)(2,1)S(1)} %fusion.41, bf16[1,1024,4096]{2,1,0:T(8,128)(2,1)} %param.12), kind=kOutput, calls=%fused_computation.22 | convolution fusion | flops 2147483648 | bytes 11534336 | tf_op jit(solution)/shard_map/tf,df->td/dot_general | solution.py:49
  224.6 5.3 %multiply_reduce_fusion.11 = f32[]{:T(128)} fusion(bf16[256,4096]{1,0:T(8,128)(2,1)S(1)} %copy-done.9, bf16[3,256,1024]{2,1,0:T(8,128)(2,1)S(1)} %copy-done.14, bf16[256]{0:T(256)(128)(2,1)S(1)} %get-tuple-element.10), kind=kOutput, calls=%fused_computation.13 | convolution fusion | flops 2156134400 | bytes 2621956 | tf_op jit(solution)/shard_map/td,tf->df/dot_general | solution.py:58
  232.5 8.1 %fusion.26 = f32[256,4096]{1,0:T(8,128)} fusion(bf16[1,1024,4096]{2,1,0:T(8,128)(2,1)} %param.12, bf16[3,256,1024]{2,1,0:T(8,128)(2,1)} %all-gather.3.cloned.1.call-done), kind=kOutput, calls=%fused_computation.36 | convolution fusion | flops 2148532224 | bytes 13107200 | tf_op jit(solution)/shard_map/dot_general | solution.py:44
  240.6 4.0 collective-permute-done.4
  244.5 1.4 add.111
  246.0 6.7 %multiply_reduce_fusion.5 = f32[]{:T(128)} fusion(bf16[256,4096]{1,0:T(8,128)(2,1)S(1)} %copy-done.12, bf16[3,256,1024]{2,1,0:T(8,128)(2,1)} %all-gather.3.cloned.1.call-done, bf16[256]{0:T(256)(128)(2,1)S(1)} %get-tuple-element.9), kind=kOutput, calls=%fused_computation.7 | convolution fusion | flops 2156134400 | bytes 2621956 | tf_op jit(solution)/shard_map/td,tf->df/dot_general | solution.py:58
  252.7 5.3 %multiply_reduce_fusion.4 = f32[]{:T(128)} fusion(bf16[256,1024]{1,0:T(8,128)(2,1)S(1)} %all_gather.14, bf16[256]{0:T(256)(128)(2,1)S(1)} %get-tuple-element.9, f32[256,4096]{1,0:T(8,128)S(1)} %copy-done.4), kind=kOutput, calls=%fused_computation.6 | convolution fusion | flops 2158231552 | bytes 4719108 | tf_op jit(solution)/shard_map/tf,td->fd/dot_general | solution.py:61
  259.3 7.6 %collective-permute-done.5 = f32[256,1024]{1,0:T(8,128)} collective-permute-done((f32[256,1024]{1,0:T(8,128)S(1)}, f32[256,1024]{1,0:T(8,128)}, u32[]{:S(2)}, u32[]{:S(2)}) %collective-permute-start.5) | collective-permute-done | bytes 1048608 | tf_op jit(solution)/shard_map/ppermute | solution.py:52
  266.9 1.4 add.112
  269.2 7.6 %multiply_reduce_fusion.7 = f32[]{:T(128)} fusion(bf16[256,4096]{1,0:T(8,128)(2,1)} %copy-done.11, bf16[3,256,1024]{2,1,0:T(8,128)(2,1)} %all-gather.3.cloned.1.call-done, bf16[256]{0:T(256)(128)(2,1)S(1)} %get-tuple-element.8), kind=kOutput, calls=%fused_computation.9 | convolution fusion | flops 2156134400 | bytes 2621956 | tf_op jit(solution)/shard_map/td,tf->df/dot_general | solution.py:58
  276.9 5.2 %multiply_reduce_fusion.6 = f32[]{:T(128)} fusion(bf16[256,1024]{1,0:T(8,128)(2,1)S(1)} %all_gather.14, bf16[256]{0:T(256)(128)(2,1)S(1)} %get-tuple-element.8, f32[256,4096]{1,0:T(8,128)S(1)} %copy-done.5), kind=kOutput, calls=%fused_computation.8 | convolution fusion | flops 2158231552 | bytes 4719108 | tf_op jit(solution)/shard_map/tf,td->fd/dot_general | solution.py:61
  283.3 26.7 %collective-permute-done.6 = f32[256,1024]{1,0:T(8,128)S(1)} collective-permute-done((f32[256,1024]{1,0:T(8,128)S(1)}, f32[256,1024]{1,0:T(8,128)S(1)}, u32[]{:S(2)}, u32[]{:S(2)}) %collective-permute-start.6) | collective-permute-done | bytes 1048608 | tf_op jit(solution)/shard_map/ppermute | solution.py:52
  311.4 1.8 collective-permute-done.7
  313.2 31.4 %all_gather.15 = bf16[256,1024]{1,0:T(8,128)(2,1)S(1)} all-gather(bf16[32,1024]{1,0:T(8,128)(2,1)S(1)} %bitcast_select_fusion), channel_id=1, replica_groups=mesh['section'=4,'tensor'=8] {'tensor'}, dimensions={0}, use_global_device_ids=true | all-gather | bytes 589824 | tf_op jit(solution)/shard_map/all_gather | solution.py:43
  344.6 7.1 %fusion.38 = bf16[256,4096]{1,0:T(8,128)(2,1)S(1)} fusion(bf16[256,1024]{1,0:T(8,128)(2,1)S(1)} %all_gather.15, bf16[1,4096,1024]{2,1,0:T(8,128)(2,1)} %param.13, f32[256,4096]{1,0:T(8,128)} %fusion.26), kind=kOutput, calls=%fused_computation.40 | convolution fusion | flops 2150629376 | bytes 15204352 | tf_op jit(solution)/shard_map/td,fd->tf/dot_general | solution.py:47
  351.7 5.3 %multiply_reduce_fusion = f32[]{:T(128)} fusion(bf16[256,1024]{1,0:T(8,128)(2,1)S(1)} %all_gather.15, bf16[256]{0:T(256)(128)(2,1)S(1)} %get-tuple-element.4, f32[256,4096]{1,0:T(8,128)S(1)} %copy-done.6), kind=kOutput, calls=%fused_computation.2 | convolution fusion | flops 2158231552 | bytes 4719108 | tf_op jit(solution)/shard_map/tf,td->fd/dot_general | solution.py:61
  357.0 5.2 %multiply_reduce_fusion.2 = f32[]{:T(128)} fusion(bf16[256,1024]{1,0:T(8,128)(2,1)S(1)} %all_gather.15, bf16[256]{0:T(256)(128)(2,1)S(1)} %get-tuple-element.3, f32[256,4096]{1,0:T(8,128)S(1)} %copy-done.6), kind=kOutput, calls=%fused_computation.4 | convolution fusion | flops 2158231552 | bytes 4719108 | tf_op jit(solution)/shard_map/tf,td->fd/dot_general | solution.py:61
  362.2 6.5 %multiply_reduce_fusion.1 = f32[]{:T(128)} fusion(bf16[256,4096]{1,0:T(8,128)(2,1)S(1)} %fusion.38, bf16[3,256,1024]{2,1,0:T(8,128)(2,1)} %all-gather.3.cloned.1.call-done, bf16[256]{0:T(256)(128)(2,1)S(1)} %get-tuple-element.4), kind=kOutput, calls=%fused_computation.3 | convolution fusion | flops 2156134400 | bytes 2621956 | tf_op jit(solution)/shard_map/td,tf->df/dot_general | solution.py:58
  370.0 6.4 %multiply_reduce_fusion.3 = f32[]{:T(128)} fusion(bf16[256,4096]{1,0:T(8,128)(2,1)S(1)} %fusion.38, bf16[3,256,1024]{2,1,0:T(8,128)(2,1)} %all-gather.3.cloned.1.call-done, bf16[256]{0:T(256)(128)(2,1)S(1)} %get-tuple-element.3), kind=kOutput, calls=%fused_computation.5 | convolution fusion | flops 2156134400 | bytes 2621956 | tf_op jit(solution)/shard_map/td,tf->df/dot_general | solution.py:58
  377.7 6.7 %fusion.6 = f32[256,1024]{1,0:T(8,128)} fusion(bf16[256,4096]{1,0:T(8,128)(2,1)S(1)} %fusion.38, bf16[1,1024,4096]{2,1,0:T(8,128)(2,1)} %param.12), kind=kOutput, calls=%fused_computation.20 | convolution fusion | flops 2147483648 | bytes 11534336 | tf_op jit(solution)/shard_map/tf,df->td/dot_general | solution.py:49
  384.5 19.8 %all-reduce = (f32[2]{0:T(128)S(1)}, f32[2]{0:T(128)S(1)}, f32[2]{0:T(128)S(1)}) all-reduce(f32[2]{0:T(128)S(1)} %pad_maximum_fusion.1, f32[2]{0:T(128)S(1)} %pad_maximum_fusion.2, f32[2]{0:T(128)S(1)} %pad_maximum_fusion.3), channel_id=1, replica_groups=mesh['section'=4,'tensor'=8] {'tensor'}, use_global_device_ids=true, to_apply=%region_5.6 | all-reduce | flops 6 | bytes 48 | tf_op jit(solution)/shard_map/psum | solution.py:66
  404.7 10.6 %fusion.53 = f32[4096,1024]{1,0:T(8,128)} fusion(bf16[256,1024]{1,0:T(8,128)(2,1)} %copy-done.7, f32[256]{0:T(256)S(1)} %select_reduce_fusion.1, f32[256,4096]{1,0:T(8,128)} %copy-done.3), kind=kOutput, calls=%fused_computation.58 | convolution fusion | flops 2150367232 | bytes 21496832 | tf_op jit(solution)/shard_map/tf,td->fd/dot_general | solution.py:74
  415.3 8.2 %fusion.52 = f32[4096,1024]{1,0:T(8,128)} fusion(bf16[1,256,1024]{2,1,0:T(8,128)(2,1)S(1)} %all-gather, f32[256]{0:T(256)S(1)} %select_reduce_fusion.2, f32[256,4096]{1,0:T(8,128)S(1)} %copy-done.2), kind=kOutput, calls=%fused_computation.57 | convolution fusion | flops 2150367232 | bytes 21496832 | tf_op jit(solution)/shard_map/tf,td->fd/dot_general | solution.py:74
  423.5 16.6 %fusion.19 = bf16[1,4096,1024]{2,1,0:T(8,128)(2,1)} fusion(f32[4096,1024]{1,0:T(8,128)} %fusion.52, f32[4096,1024]{1,0:T(8,128)} %fusion.53, bf16[256,1024]{1,0:T(8,128)(2,1)S(1)} %all_gather.15, f32[256]{0:T(256)S(1)} %select_reduce_fusion, f32[256,4096]{1,0:T(8,128)} %fusion.26), kind=kOutput, calls=%fused_computation.33 | convolution fusion | flops 2162950144 | bytes 46662656 | tf_op jit(solution)/shard_map/tf,td->fd/dot_general | solution.py:74
  440.1 1.8 add.121
  442.3 9.4 %fusion.47 = f32[1024,4096]{1,0:T(8,128)} fusion(bf16[256,4096]{1,0:T(8,128)(2,1)S(1)} %copy-done.10, f32[256]{0:T(256)S(1)} %select_reduce_fusion.2, bf16[3,256,1024]{2,1,0:T(8,128)(2,1)} %all-gather.3.cloned.1.call-done), kind=kOutput, calls=%fused_computation.49 | convolution fusion | flops 2150629376 | bytes 19399680 | tf_op jit(solution)/shard_map/td,tf->df/dot_general | solution.py:71
  451.8 9.3 %fusion.48 = f32[1024,4096]{1,0:T(8,128)} fusion(bf16[256,4096]{1,0:T(8,128)(2,1)S(1)} %copy-done.13, f32[256]{0:T(256)S(1)} %select_reduce_fusion.1, bf16[3,256,1024]{2,1,0:T(8,128)(2,1)} %all-gather.3.cloned.1.call-done), kind=kOutput, calls=%fused_computation.50 | convolution fusion | flops 2150629376 | bytes 19399680 | tf_op jit(solution)/shard_map/td,tf->df/dot_general | solution.py:71
  462.3 15.6 %fusion.18 = bf16[1,1024,4096]{2,1,0:T(8,128)(2,1)} fusion(f32[1024,4096]{1,0:T(8,128)} %fusion.47, f32[1024,4096]{1,0:T(8,128)} %fusion.48, bf16[256,4096]{1,0:T(8,128)(2,1)S(1)} %fusion.38, f32[256]{0:T(256)S(1)} %select_reduce_fusion, bf16[3,256,1024]{2,1,0:T(8,128)(2,1)} %all-gather.3.cloned.1.call-done), kind=kOutput, calls=%fused_computation.32 | convolution fusion | flops 2163212288 | bytes 44565504 | tf_op jit(solution)/shard_map/td,tf->df/dot_general | solution.py:71
  478.0 25.2 %collective-permute-done.10 = f32[256,1024]{1,0:T(8,128)} collective-permute-done((f32[256,1024]{1,0:T(8,128)}, f32[256,1024]{1,0:T(8,128)}, u32[]{:S(2)}, u32[]{:S(2)}) %collective-permute-start.10) | collective-permute-done | bytes 1048608 | tf_op jit(solution)/shard_map/ppermute | solution.py:52
  (95 shorter events, 10.9 us)
Async XLA Ops:
  7.2 56.7 %all-gather.3.cloned.1.call-start = ((), (), s32[]{:S(2)}) async-start(), calls=%async_computation | async-start | bytes 1769472 | tf_op jit(solution)/shard_map/all_gather | solution.py:36
  63.9 13.5 %slice-start.2 = ((s8[8388608]{0:T(1024)(128)(4,1)}), s8[4194304]{0:T(1024)(128)(4,1)S(1)}, s32[]{:S(2)}) async-start(s8[8388608]{0:T(1024)(128)(4,1)} %bitcast.138), calls=%async_computation.3 | async-start | bytes 8388608
  70.0 7.4 %copy-start = (f32[256,4096]{1,0:T(8,128)}, f32[256,4096]{1,0:T(8,128)S(1)}, u32[]{:S(2)}) copy-start(f32[256,4096]{1,0:T(8,128)S(1)} %fusion.20) | copy-start | bytes 12582916
  70.0 7.4 %slice-start.3 = ((s8[8388608]{0:T(1024)(128)(4,1)}), s8[4194304]{0:T(1024)(128)(4,1)S(1)}, s32[]{:S(2)}) async-start(s8[8388608]{0:T(1024)(128)(4,1)} %bitcast.138), calls=%async_computation.4 | async-start | bytes 8388608
  77.4 99.7 %copy-start.8 = (bf16[256,4096]{1,0:T(8,128)(2,1)}, bf16[256,4096]{1,0:T(8,128)(2,1)S(1)}, u32[]{:S(2)}) copy-start(bf16[256,4096]{1,0:T(8,128)(2,1)S(1)} %fusion.44) | copy-start | bytes 6291460
  77.4 4.0 copy-start.17
  80.8 24.2 %collective-permute-start = (f32[256,1024]{1,0:T(8,128)}, f32[256,1024]{1,0:T(8,128)}, u32[]{:S(2)}, u32[]{:S(2)}) collective-permute-start(f32[256,1024]{1,0:T(8,128)} %fusion.12), channel_id=1, source_target_pairs={{0,1},{1,0},{2,3},{3,2},{4,5},{5,4},{6,7},{7,6},{8,9},{9,8},{10,11... | collective-permute-start | bytes 3145736 | tf_op jit(solution)/shard_map/ppermute | solution.py:52
  106.7 23.1 %collective-permute-start.1 = (f32[256,1024]{1,0:T(8,128)S(1)}, f32[256,1024]{1,0:T(8,128)S(1)}, u32[]{:S(2)}, u32[]{:S(2)}) collective-permute-start(f32[256,1024]{1,0:T(8,128)S(1)} %add.102), channel_id=1, source_target_pairs={{0,2},{1,3},{2,0},{3,1},{4,6},{5,7},{6,4},{7,5},{8,10},{9,11},{10,... | collective-permute-start | bytes 3145736 | tf_op jit(solution)/shard_map/ppermute | solution.py:52
  108.1 24.3 %copy-start.1 = (f32[256,4096]{1,0:T(8,128)S(1)}, f32[256,4096]{1,0:T(8,128)}, u32[]{:S(2)}) copy-start(f32[256,4096]{1,0:T(8,128)} %copy-done) | copy-start | bytes 12582916
  129.8 8.1 %slice-start.4 = ((s8[8388608]{0:T(1024)(128)(4,1)}), s8[4194304]{0:T(1024)(128)(4,1)S(1)}, s32[]{:S(2)}) async-start(s8[8388608]{0:T(1024)(128)(4,1)} %bitcast.140), calls=%async_computation.5 | async-start | bytes 8388608
  129.9 45.6 %collective-permute-start.2 = (f32[256,1024]{1,0:T(8,128)S(1)}, f32[256,1024]{1,0:T(8,128)S(1)}, u32[]{:S(2)}, u32[]{:S(2)}) collective-permute-start(f32[256,1024]{1,0:T(8,128)S(1)} %add.103), channel_id=1, source_target_pairs={{0,4},{1,5},{2,6},{3,7},{4,0},{5,1},{6,2},{7,3},{8,12},{9,13},{10,... | collective-permute-start | bytes 3145736 | tf_op jit(solution)/shard_map/ppermute | solution.py:52
  132.3 5.5 %copy-start.14 = (bf16[3,256,1024]{2,1,0:T(8,128)(2,1)S(1)}, bf16[3,256,1024]{2,1,0:T(8,128)(2,1)}, u32[]{:S(2)}) copy-start(bf16[3,256,1024]{2,1,0:T(8,128)(2,1)} %all-gather.3.cloned.1.call-done) | copy-start | bytes 4718596
  132.3 5.5 %slice-start.5 = ((s8[8388608]{0:T(1024)(128)(4,1)}), s8[4194304]{0:T(1024)(128)(4,1)S(1)}, s32[]{:S(2)}) async-start(s8[8388608]{0:T(1024)(128)(4,1)} %bitcast.140), calls=%async_computation.6 | async-start | bytes 8388608
  137.8 37.7 %copy-start.15 = (bf16[1,32,1024]{2,1,0:T(8,128)(2,1)S(1)}, bf16[1,32,1024]{2,1,0:T(8,128)(2,1)}, u32[]{:S(2)}) copy-start(bf16[1,32,1024]{2,1,0:T(8,128)(2,1)} %param.10) | copy-start | bytes 196612
  140.3 74.0 %copy-start.3 = (f32[256,4096]{1,0:T(8,128)}, f32[256,4096]{1,0:T(8,128)S(1)}, u32[]{:S(2)}) copy-start(f32[256,4096]{1,0:T(8,128)S(1)} %fusion.23) | copy-start | bytes 12582916
  175.5 38.8 %slice-start = ((s8[8388608]{0:T(1024)(128)(4,1)}), s8[4194304]{0:T(1024)(128)(4,1)S(1)}, s32[]{:S(2)}) async-start(s8[8388608]{0:T(1024)(128)(4,1)} %bitcast.136), calls=%async_computation.1 | async-start | bytes 8388608
  175.6 6.9 %copy-start.16 = (bf16[2,32,1024]{2,1,0:T(8,128)(2,1)S(1)}, bf16[2,32,1024]{2,1,0:T(8,128)(2,1)}, u32[]{:S(2)}) copy-start(bf16[2,32,1024]{2,1,0:T(8,128)(2,1)} %param.11) | copy-start | bytes 393220
  175.6 38.8 %slice-start.1 = ((s8[8388608]{0:T(1024)(128)(4,1)}), s8[4194304]{0:T(1024)(128)(4,1)S(1)}, s32[]{:S(2)}) async-start(s8[8388608]{0:T(1024)(128)(4,1)} %bitcast.136), calls=%async_computation.2 | async-start | bytes 8388608
  175.6 6.8 %collective-permute-start.3 = (bf16[32,1024]{1,0:T(8,128)(2,1)S(1)}, bf16[32,1024]{1,0:T(8,128)(2,1)S(1)}, u32[]{:S(2)}, u32[]{:S(2)}) collective-permute-start(bf16[32,1024]{1,0:T(8,128)(2,1)S(1)} %fusion.86), channel_id=1, source_target_pairs={{8,0},{16,8},{24,16},{9,1},{17,9},{25,17},{10,2},{18,10},{26,18},{... | collective-permute-start | bytes 196616 | tf_op jit(solution)/shard_map/ppermute | solution.py:14
  214.4 62.5 %copy-start.7 = (bf16[256,1024]{1,0:T(8,128)(2,1)}, bf16[256,1024]{1,0:T(8,128)(2,1)S(1)}, u32[]{:S(2)}) copy-start(bf16[256,1024]{1,0:T(8,128)(2,1)S(1)} %all_gather.14) | copy-start | bytes 1572868
  216.9 6.6 %copy-start.11 = (bf16[256,4096]{1,0:T(8,128)(2,1)}, bf16[256,4096]{1,0:T(8,128)(2,1)S(1)}, u32[]{:S(2)}) copy-start(bf16[256,4096]{1,0:T(8,128)(2,1)S(1)} %fusion.41) | copy-start | bytes 6291460
  216.9 7.7 %copy-start.9 = (bf16[256,4096]{1,0:T(8,128)(2,1)S(1)}, bf16[256,4096]{1,0:T(8,128)(2,1)}, u32[]{:S(2)}) copy-start(bf16[256,4096]{1,0:T(8,128)(2,1)} %copy-done.8) | copy-start | bytes 6291460
  223.5 21.0 %collective-permute-start.4 = (f32[256,1024]{1,0:T(8,128)S(1)}, f32[256,1024]{1,0:T(8,128)}, u32[]{:S(2)}, u32[]{:S(2)}) collective-permute-start(f32[256,1024]{1,0:T(8,128)S(1)} %fusion.8), channel_id=1, source_target_pairs={{0,1},{1,0},{2,3},{3,2},{4,5},{5,4},{6,7},{7,6},{8,9},{9,8},{10,11... | collective-permute-start | bytes 3145736 | tf_op jit(solution)/shard_map/ppermute | solution.py:52
  232.5 13.5 %copy-start.12 = (bf16[256,4096]{1,0:T(8,128)(2,1)S(1)}, bf16[256,4096]{1,0:T(8,128)(2,1)}, u32[]{:S(2)}) copy-start(bf16[256,4096]{1,0:T(8,128)(2,1)} %copy-done.11) | copy-start | bytes 6291460
  245.9 21.1 %collective-permute-start.5 = (f32[256,1024]{1,0:T(8,128)S(1)}, f32[256,1024]{1,0:T(8,128)}, u32[]{:S(2)}, u32[]{:S(2)}) collective-permute-start(f32[256,1024]{1,0:T(8,128)S(1)} %add.111), channel_id=1, source_target_pairs={{0,2},{1,3},{2,0},{3,1},{4,6},{5,7},{6,4},{7,5},{8,10},{9,11},{10,... | collective-permute-start | bytes 3145736 | tf_op jit(solution)/shard_map/ppermute | solution.py:52
  246.0 6.8 %copy-start.4 = (f32[256,4096]{1,0:T(8,128)S(1)}, f32[256,4096]{1,0:T(8,128)}, u32[]{:S(2)}) copy-start(f32[256,4096]{1,0:T(8,128)} %copy-done.3) | copy-start | bytes 12582916
  268.3 41.7 %collective-permute-start.6 = (f32[256,1024]{1,0:T(8,128)S(1)}, f32[256,1024]{1,0:T(8,128)S(1)}, u32[]{:S(2)}, u32[]{:S(2)}) collective-permute-start(f32[256,1024]{1,0:T(8,128)S(1)} %add.112), channel_id=1, source_target_pairs={{0,4},{1,5},{2,6},{3,7},{4,0},{5,1},{6,2},{7,3},{8,12},{9,13},{10,... | collective-permute-start | bytes 3145736 | tf_op jit(solution)/shard_map/ppermute | solution.py:52
  269.2 7.6 %copy-start.5 = (f32[256,4096]{1,0:T(8,128)S(1)}, f32[256,4096]{1,0:T(8,128)}, u32[]{:S(2)}) copy-start(f32[256,4096]{1,0:T(8,128)} %copy-done.3) | copy-start | bytes 12582916
  310.0 3.1 collective-permute-start.7
  344.6 7.1 %copy-start.6 = (f32[256,4096]{1,0:T(8,128)S(1)}, f32[256,4096]{1,0:T(8,128)}, u32[]{:S(2)}) copy-start(f32[256,4096]{1,0:T(8,128)} %fusion.26) | copy-start | bytes 12582916
  404.6 10.7 %copy-start.2 = (f32[256,4096]{1,0:T(8,128)S(1)}, f32[256,4096]{1,0:T(8,128)}, u32[]{:S(2)}) copy-start(f32[256,4096]{1,0:T(8,128)} %copy-done) | copy-start | bytes 12582916
  404.6 35.5 %collective-permute-start.8 = (f32[256,1024]{1,0:T(8,128)}, f32[256,1024]{1,0:T(8,128)}, u32[]{:S(2)}, u32[]{:S(2)}) collective-permute-start(f32[256,1024]{1,0:T(8,128)} %fusion.6), channel_id=1, source_target_pairs={{0,1},{1,0},{2,3},{3,2},{4,5},{5,4},{6,7},{7,6},{8,9},{9,8},{10,11... | collective-permute-start | bytes 3145736 | tf_op jit(solution)/shard_map/ppermute | solution.py:52
  440.1 2.2 copy-start.10
  442.0 9.8 %copy-start.13 = (bf16[256,4096]{1,0:T(8,128)(2,1)S(1)}, bf16[256,4096]{1,0:T(8,128)(2,1)}, u32[]{:S(2)}) copy-start(bf16[256,4096]{1,0:T(8,128)(2,1)} %copy-done.11) | copy-start | bytes 6291460
  442.0 19.0 %collective-permute-start.9 = (f32[256,1024]{1,0:T(8,128)S(1)}, f32[256,1024]{1,0:T(8,128)S(1)}, u32[]{:S(2)}, u32[]{:S(2)}) collective-permute-start(f32[256,1024]{1,0:T(8,128)S(1)} %add.121), channel_id=1, source_target_pairs={{0,2},{1,3},{2,0},{3,1},{4,6},{5,7},{6,4},{7,5},{8,10},{9,11},{10,... | collective-permute-start | bytes 3145736 | tf_op jit(solution)/shard_map/ppermute | solution.py:52
  462.2 41.0 %collective-permute-start.10 = (f32[256,1024]{1,0:T(8,128)}, f32[256,1024]{1,0:T(8,128)}, u32[]{:S(2)}, u32[]{:S(2)}) collective-permute-start(f32[256,1024]{1,0:T(8,128)} %add.122), channel_id=1, source_target_pairs={{0,4},{1,5},{2,6},{3,7},{4,0},{5,1},{6,2},{7,3},{8,12},{9,13},{10,... | collective-permute-start | bytes 3145736 | tf_op jit(solution)/shard_map/ppermute | solution.py:52
Sparse Core Ops, SparseCore 0:
  16.2 47.6 all-gather.2
